TPU v7x, 32 devices: a 4x4x1 block of a 4x4x8 slice. The times are simulated.
32 devices in a mesh: dp: 1 (over z), ep2: 4 (over y), ep: 8 (over x, core).
Axes of the slice: x: 4, y: 4, z: 1, core: 2. Of those that a mesh axis runs over, the one named last changes fastest.
The devices are a block of a 4x4x8 slice.
Arguments:
- tokens: bfloat16 [4096, 2560], P(('dp', 'ep2', 'ep'))
- expert_ids: int32 [4096, 6], P(('dp', 'ep2', 'ep'))
- gates: float32 [4096, 6], P(('dp', 'ep2', 'ep'))
- w_gate: bfloat16 [64, 2560, 1536], P(('ep2', 'ep'))
- w_up: bfloat16 [64, 2560, 1536], P(('ep2', 'ep'))
- w_down: bfloat16 [64, 1536, 2560], P(('ep2', 'ep'))
Outputs:
- output: bfloat16 [4096, 2560], P(('dp', 'ep2', 'ep'))
All inputs are finite; a program needn't handle non-finite values.
Results may differ from a plain program's by a relative error of at most 0.001.
Values are sent between devices in bfloat16 or wider.
A program may use at most 768 MiB of HBM per device.

v0:
```python
import jax
import jax.numpy as jnp
from jax import lax
from jax.sharding import PartitionSpec as P


def slot_matrix(expert_ids, n_expert, row_cap):
    n_tok, n_top = expert_ids.shape
    flat_ids = expert_ids.reshape(n_tok * n_top)
    expert_hot = (flat_ids[:, None] == jnp.arange(n_expert)[None, :]).astype(jnp.int32)
    running = jnp.cumsum(expert_hot, axis=0)
    slot_pos = jnp.sum(expert_hot * running, axis=1) - 1
    dest_pos = flat_ids * row_cap + slot_pos
    slot_hot = dest_pos[:, None] == jnp.arange(n_expert * row_cap)[None, :]
    return slot_hot.reshape(n_tok, n_top, n_expert * row_cap).astype(jnp.bfloat16)


def expert_ffn(rows_in, w_gate, w_up, w_down):
    act_gate = jnp.einsum('slcd,ldf->slcf', rows_in, w_gate, preferred_element_type=jnp.float32)
    act_up = jnp.einsum('slcd,ldf->slcf', rows_in, w_up, preferred_element_type=jnp.float32)
    hidden = (jax.nn.silu(act_gate) * act_up).astype(jnp.bfloat16)
    return jnp.einsum('slcf,lfd->slcd', hidden, w_down, preferred_element_type=jnp.float32).astype(jnp.bfloat16)


def solution(mesh):
    group_axes = ('ep2', 'ep')
    n_group = mesh.shape['ep2'] * mesh.shape['ep']
    row_spec = P(('dp', 'ep2', 'ep'), None)
    weight_spec = P(group_axes, None, None)

    def device_step(tokens, expert_ids, gates, w_gate, w_up, w_down):
        n_tok, n_top = expert_ids.shape
        local_count, model_dim = w_gate.shape[0], w_gate.shape[1]
        n_expert = local_count * n_group
        row_cap = -(-(n_tok * n_top) // n_expert)
        slot_hot = slot_matrix(expert_ids, n_expert, row_cap)
        send_buf = jnp.einsum('tjp,td->pd', slot_hot, tokens, preferred_element_type=jnp.float32).astype(jnp.bfloat16)
        recv_buf = lax.all_to_all(send_buf, group_axes, 0, 0, tiled=True)
        expert_out = expert_ffn(recv_buf.reshape(n_group, local_count, row_cap, model_dim), w_gate, w_up, w_down)
        back_buf = lax.all_to_all(expert_out.reshape(n_expert * row_cap, model_dim), group_axes, 0, 0, tiled=True)
        picked = jnp.einsum('tjp,pd->tjd', slot_hot, back_buf, preferred_element_type=jnp.float32)
        total = tokens.astype(jnp.float32)
        for slot_j in range(n_top):
            total = total + gates[:, slot_j:slot_j + 1] * picked[:, slot_j]
        return total.astype(jnp.bfloat16)

    return jax.shard_map(device_step, mesh=mesh, in_specs=(row_spec, row_spec, row_spec, weight_spec, weight_spec, weight_spec), out_specs=row_spec, check_vma=False)
```

profile of v0, /device:TPU:97, one launch (start us, length us, event | category | flops | bytes accessed | tf_op | source)
XLA Modules:
  0.0 167.1 jit_solution(16764613154622342015)
XLA Ops:
  0.0 0.8 copy.35
  0.8 0.1 eq.64
  0.9 0.1 eq.60
  1.1 1.8 %reduce-window.6 = s32[64,6,128]{2,0,1:T(8,128)S(1)} reduce-window(s32[64,6,128]{2,0,1:T(8,128)S(1)} %fusion.38, s32[]{:T(128)} %constant.12.clone.1), window={size=1x1x128 pad=0_0x0_0x127_0}, to_apply=%region_0.0 | reduce-window | flops 6242304 | bytes 393220 | tf_op jit(solution)/shard_map/reduce-window
  2.9 0.3 slice_reduce_fusion
  3.2 0.1 fusion.37
  3.4 0.1 sub.7
  3.5 0.1 copy.38
  3.5 0.7 multiply_add_fusion
  4.3 0.3 convert_reduce_fusion
  4.6 2.3 %fusion.40 = bf16[768,2560]{1,0:T(8,128)(2,1)S(1)} fusion(bf16[128,768]{1,0:T(8,128)(2,1)S(1)} %convert_reduce_fusion, bf16[128,2560]{1,0:T(8,128)(2,1)} %param.6), kind=kOutput, calls=%fused_computation.59 | convolution fusion | flops 503316480 | bytes 4784128 | tf_op jit(solution)/shard_map/tjp,td->pd/dot_general | solution.py:37
  6.9 0.0 copy-start.3
  6.9 58.9 %all_to_all.21 = bf16[32,24,2560]{2,1,0:T(8,128)(2,1)S(1)} all-to-all(bf16[32,24,2560]{2,1,0:T(8,128)(2,1)S(1)} %bitcast.134), channel_id=1, replica_groups=mesh['dp'=1,'ep2'=4,'ep'=8] {'ep2','ep'}, dimensions={0} | all-to-all | bytes 7864320 | tf_op jit(solution)/shard_map/all_to_all | solution.py:38
  65.8 1.2 copy.39
  67.0 0.0 copy-start
  67.0 1.9 %copy-done = bf16[32,24,2560]{2,0,1:T(8,128)(2,1)} copy-done((bf16[32,24,2560]{2,0,1:T(8,128)(2,1)}, bf16[32,24,2560]{2,0,1:T(8,128)(2,1)S(1)}, u32[]{:S(2)}) %copy-start) | copy-done | bytes 3932184
  68.8 0.0 copy-done.3
  68.8 7.8 %fusion.4 = f32[2,32,12,1536]{3,1,2,0:T(8,128)} fusion(bf16[32,2,12,2560]{3,0,2,1:T(8,128)(2,1)S(1)} %bitcast.135, bf16[2,2560,1536]{2,1,0:T(8,128)(2,1)S(1)} %copy-done.3), kind=kOutput, calls=%fused_computation.4 | convolution fusion | flops 6039797760 | bytes 24379392 | tf_op jit(solution)/shard_map/slcd,ldf->slcf/dot_general | solution.py:19
  76.6 20.6 %fusion.6 = bf16[2,32,12,2560]{3,1,2,0:T(8,128)(2,1)} fusion(bf16[2,1536,2560]{2,1,0:T(8,128)(2,1)} %param.11, f32[2,32,12,1536]{3,1,2,0:T(8,128)} %fusion.4, bf16[32,2,12,2560]{3,0,2,1:T(8,128)(2,1)} %bitcast.136, bf16[2,2560,1536]{2,1,0:T(8,128)(2,1)} %param.10), kind=kOutput, calls=%fused_computation.6 | convolution fusion | flops 12088639488 | bytes 44040192 | tf_op jit(solution)/shard_map/slcf,lfd->slcd/dot_general | solution.py:22
  97.3 6.1 %copy.40 = bf16[32,24,2560]{2,1,0:T(8,128)(2,1)} copy(bf16[32,24,2560]{2,0,1:T(8,128)(2,1)} %bitcast.137) | data formatting | bytes 7864320 | tf_op jit(solution)/shard_map/all_to_all | solution.py:40
  103.4 0.0 copy-start.2
  103.4 5.0 %all-to-all-start.1 = ((bf16[32,24,2560]{2,1,0:T(8,128)(2,1)}), bf16[32,24,2560]{2,1,0:T(8,128)(2,1)}, u32[]{:S(2)}, u32[]{:S(2)}) async-start(bf16[32,24,2560]{2,1,0:T(8,128)(2,1)} %copy.40), calls=%async_computation.1 | async-start | bytes 7864320 | tf_op jit(solution)/shard_map/all_to_all | solution.py:40
  108.4 0.0 copy-done.2
  108.5 51.5 %all-to-all-done.1 = bf16[32,24,2560]{2,1,0:T(8,128)(2,1)} async-done(((bf16[32,24,2560]{2,1,0:T(8,128)(2,1)}), bf16[32,24,2560]{2,1,0:T(8,128)(2,1)}, u32[]{:S(2)}, u32[]{:S(2)}) %all-to-all-start.1) | async-done | bytes 3932192 | tf_op jit(solution)/shard_map/all_to_all | solution.py:40
  160.0 0.0 copy-start.1
  160.0 5.4 %fusion.19 = f32[128,6,2560]{2,0,1:T(8,128)S(1)} fusion(bf16[768,2560,1]{1,0,2:T(8,128)(2,1)} %bitcast.16, s32[128,6]{0,1:T(8,128)S(1)} %multiply_add_fusion), kind=kOutput, calls=%fused_computation.20 | convolution fusion | flops 3020488704 | bytes 11799552 | tf_op jit(solution)/shard_map/tjp,pd->tjd/dot_general | solution.py:41
  165.5 0.0 copy-done.1
  165.5 1.6 fusion.24
  (4 shorter events, 0.1 us)
Async XLA Ops:
  6.9 62.0 %copy-start.3 = (bf16[2,2560,1536]{2,1,0:T(8,128)(2,1)S(1)}, bf16[2,2560,1536]{2,1,0:T(8,128)(2,1)}, u32[]{:S(2)}) copy-start(bf16[2,2560,1536]{2,1,0:T(8,128)(2,1)} %param.9) | copy-start | bytes 47185924
  67.0 1.9 %copy-start = (bf16[32,24,2560]{2,0,1:T(8,128)(2,1)}, bf16[32,24,2560]{2,0,1:T(8,128)(2,1)S(1)}, u32[]{:S(2)}) copy-start(bf16[32,24,2560]{2,0,1:T(8,128)(2,1)S(1)} %copy.39) | copy-start | bytes 11796484
  103.4 5.0 %copy-start.2 = (f32[128,6]{0,1:T(8,128)S(1)}, f32[128,6]{0,1:T(8,128)}, u32[]{:S(2)}) copy-start(f32[128,6]{0,1:T(8,128)} %param.8) | copy-start | bytes 9220
  103.4 56.6 %all-to-all-start.1 = ((bf16[32,24,2560]{2,1,0:T(8,128)(2,1)}), bf16[32,24,2560]{2,1,0:T(8,128)(2,1)}, u32[]{:S(2)}, u32[]{:S(2)}) async-start(bf16[32,24,2560]{2,1,0:T(8,128)(2,1)} %copy.40), calls=%async_computation.1 | async-start | bytes 7864320 | tf_op jit(solution)/shard_map/all_to_all | solution.py:40
  160.0 5.5 %copy-start.1 = (bf16[128,2560]{1,0:T(8,128)(2,1)S(1)}, bf16[128,2560]{1,0:T(8,128)(2,1)}, u32[]{:S(2)}) copy-start(bf16[128,2560]{1,0:T(8,128)(2,1)} %param.6) | copy-start | bytes 1966084
where the time goes:
time: 168 us; the launch traced here: 167 us
  blocking collectives  58.9 us (35%)
  waiting for transfers between devices  51.5 us (31%)
  matrix products  36.2 us (22%)
  local copies, waits for them, and re-layouts  10.7 us (6%)
  starting transfers between devices  5.01 us (3%)
  other arithmetic  4.62 us (3%)
    all_to_all x1, blocking collectives, device_step(): recv_buf = lax.all_to_all(send_buf, group_axes, 0, 0, tiled=True)  58.9 us
    all_to_all x1, waiting for transfers between devices, device_step(): lax.all_to_all(expert_out.reshape(n_expert * row_cap, model_dim), group_a...  51.5 us
    dot_general x1, matrix products, expert_ffn(): jnp.einsum('slcf,lfd->slcd', hidden, w_down, preferred_element_type=jnp.f...  20.6 us
    dot_general x1, matrix products, expert_ffn(): jnp.einsum('slcd,ldf->slcf', rows_in, w_gate, preferred_element_type=jnp....  7.8 us
    all_to_all x1, local copies, waits for them, and re-layouts, device_step(): lax.all_to_all(expert_out.reshape(n_expert * row_cap, model_dim), group_a...  6.14 us
    dot_general x1, matrix products, device_step(): jnp.einsum('tjp,pd->tjd', slot_hot, back_buf, preferred_element_type=jnp....  5.44 us
    all_to_all x1, starting transfers between devices, device_step(): lax.all_to_all(expert_out.reshape(n_expert * row_cap, model_dim), group_a...  5.01 us
  transfers between devices with their start and end apart: 1, of which 1 were waited for; matrix products, arithmetic and copies ran while one was open for 0% of the time, Pallas kernels for 0%

commit v1 on v0

v1 whole, which is shorter than its diff:
```python
import functools

import jax
import jax.numpy as jnp
from jax import lax
from jax.experimental import pallas as pl
from jax.experimental.pallas import tpu as pltpu
from jax.sharding import PartitionSpec as P

MESH = pl.DeviceIdType.MESH
F32 = jnp.float32
BF16 = jnp.bfloat16
PEERS = [(1, 0), (3, 0), (1, 1), (3, 1), (2, 0), (2, 1), (0, 1)]
MATES = [1, 3, 2]


def div12(v):
    return (v * 2731) >> 15


def nt_dot(a, b):
    return lax.dot_general(a, b, (((1,), (1,)), ((), ())), preferred_element_type=F32)


def dot(a, b):
    return jnp.dot(a, b, preferred_element_type=F32)


def moe_kernel(
    n_line, cap, n_half, n_chunk, f_tile,
    x_ref, idx_ref, gate_ref, w1_hbm, w3_hbm, w2_hbm, out_ref,
    w1, w3, w2, mts, m_own, xg, sel, sendb, rows, hid, y1, y3, perm, gmat, acc,
    w13_sem, w2_sem, mt_s, mt_r, g_s, g_r, d_s, d_r, c_s, c_r, e_s, e_r,
):
    n_tok, dim = x_ref.shape
    n_top = idx_ref.shape[1]
    n_loc, ffn = w2_hbm.shape[0], w2_hbm.shape[1]
    n_exp = mts.shape[1]
    per = n_line * cap
    n_rows = 2 * n_line * per
    n_w2 = w2.shape[0]
    half = dim // n_half
    wide = dim // n_chunk

    dp = lax.axis_index('dp')
    yy = lax.axis_index('ep2')
    ee = lax.axis_index('ep')
    xx = ee // 2
    cc = lax.rem(ee, 2)
    k_self = jnp.where(cc == 0, yy, xx)
    q_self = jnp.where(cc == 0, xx, yy)
    i_self = cc * n_line + q_self
    d_self = 2 * q_self + cc
    coef_k = jnp.where(cc == 0, 16, 4)
    coef_q = jnp.where(cc == 0, 4, 16)

    def mod(v):
        return lax.rem(v + n_line, n_line)

    def mate(m):
        k = mod(k_self + m)
        return (dp, jnp.where(cc == 0, k, yy), jnp.where(cc == 0, xx, k) * 2 + cc)

    def spread_peer(m, dc):
        q = mod(q_self + m)
        c2 = lax.rem(cc + dc, 2)
        dev = (dp, jnp.where(cc == 0, yy, q), jnp.where(cc == 0, q, xx) * 2 + c2)
        return dev, 2 * q + c2

    def rows_at(start, size, unit):
        return pl.ds(pl.multiple_of(start, unit), size)

    def half_cols(h):
        return pl.ds(h * half, half)

    def cols_at(c):
        return pl.ds(pl.multiple_of(c * wide, wide), wide)

    def w13_copy(which, l):
        hbm, buf = ((w1_hbm, w1), (w3_hbm, w3))[which]
        return pltpu.make_async_copy(hbm.at[l], buf.at[l], w13_sem.at[which, l])

    def w2_copy(t):
        slot = lax.rem(t, n_w2)
        return pltpu.make_async_copy(
            w2_hbm.at[t // n_chunk, :, cols_at(lax.rem(t, n_chunk))], w2.at[slot], w2_sem.at[slot])

    def mt_copy(m):
        return pltpu.make_async_remote_copy(
            mts.at[k_self], mts.at[k_self], mt_s.at[m - 1], mt_r.at[m - 1], device_id=mate(m), device_id_type=MESH)

    def gather_copy(m, h):
        return pltpu.make_async_remote_copy(
            x_ref.at[:, half_cols(h)], xg.at[rows_at(k_self * n_tok, n_tok, 8), half_cols(h)],
            g_s.at[m - 1, h], g_r.at[m - 1, h], device_id=mate(m), device_id_type=MESH)

    def spread_copy(l, h, m, dc):
        dev, d = spread_peer(m, dc)
        return pltpu.make_async_remote_copy(
            sendb.at[l, rows_at(d * per, per, 8), half_cols(h)],
            rows.at[l, rows_at(i_self * per, per, 8), half_cols(h)],
            d_s.at[l, h, d], d_r.at[l, h, i_self], device_id=dev, device_id_type=MESH)

    def spread_wait(l, h):
        for o in range(1, 2 * n_line):
            i = lax.rem(i_self + o, 2 * n_line)
            pltpu.make_async_remote_copy(
                sendb.at[l, rows_at(i * per, per, 8), half_cols(h)],
                rows.at[l, rows_at(i * per, per, 8), half_cols(h)],
                d_s.at[l, h, i], d_r.at[l, h, i], device_id=mate(1), device_id_type=MESH).wait_recv()

    def back_targets():
        out = []
        for m in (1, 3, 2):
            for side in (0, 1):
                pos = mod((yy if side else xx) + m)
                dev = (dp, pos, xx * 2 + 1) if side else (dp, yy, pos * 2)
                d_me = 2 * (yy if side else xx) + cc
                out.append((side * n_line + pos, dev, d_me))
        other = 1 - cc
        pos = jnp.where(other == 0, xx, yy)
        out.append((other * n_line + pos, (dp, yy, xx * 2 + other), 2 * pos + cc))
        return out

    def back_copies(l, c):
        return [
            pltpu.make_async_remote_copy(
                rows.at[l, rows_at(i * per, per, 8), cols_at(c)], y1.at[l, rows_at(d_me * per, per, 8), cols_at(c)],
                c_s.at[l, c, i], c_r.at[l, c, d_me], device_id=dev, device_id_type=MESH)
            for i, dev, d_me in back_targets()
        ]

    def back_wait(l, c):
        for o in range(1, 2 * n_line):
            d = lax.rem(d_self + o, 2 * n_line)
            pltpu.make_async_remote_copy(
                rows.at[l, rows_at(d * per, per, 8), cols_at(c)], y1.at[l, rows_at(d * per, per, 8), cols_at(c)],
                c_s.at[l, c, d], c_r.at[l, c, d], device_id=mate(1), device_id_type=MESH).wait_recv()

    home = 2 * n_line * cap

    def home_copy(l, c, m):
        s = mod(k_self + m)
        return pltpu.make_async_remote_copy(
            sendb.at[l, rows_at(s * home, home, 8), cols_at(c)], y3.at[l, rows_at(k_self * home, home, 8), cols_at(c)],
            e_s.at[l, c, m - 1], e_r.at[l, c, m - 1], device_id=mate(m), device_id_type=MESH)

    for l in range(n_loc):
        for which in range(2):
            w13_copy(which, l).start()
    for t in range(n_w2):
        w2_copy(t).start()

    barrier = pltpu.get_barrier_semaphore()
    for side in (0, 1):
        for m in range(n_line):
            for dc in (0, 1):
                if (m, dc) == (0, 0) or (side and m == 0):
                    continue
                pos = mod((yy if side else xx) + m)
                c2 = lax.rem(cc + dc, 2)
                dev = (dp, pos, xx * 2 + c2) if side else (dp, yy, pos * 2 + c2)
                pl.semaphore_signal(barrier, inc=1, device_id=dev, device_id_type=MESH)

    lane_e = lax.broadcasted_iota(jnp.int32, (n_tok, n_exp), 1)
    chosen = jnp.zeros((n_tok, n_exp), F32)
    for j in range(n_top):
        chosen = chosen + (idx_ref[:, j:j + 1] == lane_e).astype(F32)
    lower = (lax.broadcasted_iota(jnp.int32, (n_tok, n_tok), 1)
             < lax.broadcasted_iota(jnp.int32, (n_tok, n_tok), 0)).astype(BF16)
    slot = dot(lower, chosen.astype(BF16))
    slot = jnp.where(chosen > 0, slot, -1.0).astype(BF16)
    m_own[...] = slot
    eye = (lax.broadcasted_iota(jnp.int32, (n_exp, n_exp), 0)
           == lax.broadcasted_iota(jnp.int32, (n_exp, n_exp), 1)).astype(BF16)
    mts[k_self] = nt_dot(eye, slot).astype(BF16)

    pl.semaphore_wait(barrier, 4 * n_line - 3)

    for m in MATES:
        mt_copy(m).start()
    for h in range(n_half):
        for m in MATES:
            gather_copy(m, h).start()

    xg[rows_at(k_self * n_tok, n_tok, 8), :] = x_ref[...]

    r = lax.broadcasted_iota(jnp.int32, (n_rows, 1), 0)
    r12 = div12(r)
    r_slot = (r - r12 * cap).astype(F32)
    r_src = r12 & (n_line - 1)
    r_dev = r12 >> 2
    r_exp0 = coef_k * k_self + coef_q * (r_dev >> 1) + 2 * (r_dev & 1)
    e_lane = lax.broadcasted_iota(jnp.int32, (n_rows, n_exp), 1)
    for m in MATES:
        mt_copy(m).wait_recv()
    for l in range(n_loc):
        pick = (e_lane == r_exp0 + l).astype(BF16)
        for s in range(n_line):
            val = dot(pick, mts[s])
            hit = jnp.logical_and(val == r_slot, r_src == s)
            sel[l, :, s * n_tok:(s + 1) * n_tok] = jnp.where(hit, 1.0, 0.0).astype(BF16)

    def spread(l, h):
        sendb[l, :, half_cols(h)] = dot(sel[l], xg[:, half_cols(h)]).astype(BF16)
        for m, dc in PEERS:
            spread_copy(l, h, m, dc).start()
        rows[l, rows_at(i_self * per, per, 8), half_cols(h)] = sendb[l, rows_at(d_self * per, per, 8), half_cols(h)]

    for h in range(n_half):
        for m in MATES:
            gather_copy(m, h).wait_recv()
        spread(0, h)
    for h in range(n_half):
        for l in range(1, n_loc):
            spread(l, h)

    o12 = r12
    o_in = (o12 & 7) * per + (o12 >> 3) * cap + (r - r12 * cap)
    perm[...] = (lax.broadcasted_iota(jnp.int32, (n_rows, n_rows), 1) == o_in).astype(BF16)

    gate = jnp.zeros((n_tok, n_exp), F32)
    for j in range(n_top):
        gate = gate + jnp.where(idx_ref[:, j:j + 1] == lane_e, gate_ref[:, j:j + 1], 0.0)
    parts = []
    rest = gate
    for _ in range(3):
        part = rest.astype(BF16)
        parts.append(part)
        rest = rest - part.astype(F32)
    q = lax.broadcasted_iota(jnp.int32, (1, n_rows), 1)
    q12 = div12(q)
    q_slot = (q - q12 * cap).astype(F32)
    q_dev = q12 & 7
    q_exp0 = coef_k * (q12 >> 3) + coef_q * (q_dev >> 1) + 2 * (q_dev & 1)
    e_row = lax.broadcasted_iota(jnp.int32, (n_exp, n_rows), 0)
    for l in range(n_loc):
        spread_e = (e_row == q_exp0 + l).astype(BF16)
        hit = dot(m_own[...], spread_e) == q_slot
        for p in range(3):
            gmat[l, p * n_tok:(p + 1) * n_tok, :] = jnp.where(hit, dot(parts[p], spread_e), 0.0).astype(BF16)
    acc[...] = x_ref[...].astype(F32)

    def expert_up(l):
        for h in range(n_half):
            spread_wait(l, h)
        for which in range(2):
            w13_copy(which, l).wait()

        def tile(n, carry):
            cols = pl.ds(pl.multiple_of(n * f_tile, f_tile), f_tile)
            a = dot(rows[l], w1[l, :, cols])
            b = dot(rows[l], w3[l, :, cols])
            hid[:, cols] = (jax.nn.silu(a) * b).astype(BF16)
            return carry

        lax.fori_loop(0, ffn // f_tile, tile, 0)

    def expert_down(l, c):
        t = l * n_chunk + c
        w2_copy(t).wait()
        rows[l, :, cols_at(c)] = dot(hid[...], w2[lax.rem(t, n_w2)]).astype(BF16)

        @pl.when(t + n_w2 < n_loc * n_chunk)
        def _():
            w2_copy(t + n_w2).start()

        for copy in back_copies(l, c):
            copy.start()
        y1[l, rows_at(d_self * per, per, 8), cols_at(c)] = rows[l, rows_at(i_self * per, per, 8), cols_at(c)]

    def forward(l, c):
        back_wait(l, c)
        sendb[l, :, cols_at(c)] = dot(perm[...], y1[l, :, cols_at(c)]).astype(BF16)
        for m in MATES:
            home_copy(l, c, m).start()
        y3[l, rows_at(k_self * home, home, 8), cols_at(c)] = sendb[l, rows_at(k_self * home, home, 8), cols_at(c)]

    def collect(l, c):
        for m in MATES:
            home_copy(l, c, m).wait_recv()
        part = dot(gmat[l], y3[l, :, cols_at(c)])
        acc[:, cols_at(c)] += part[:n_tok] + part[n_tok:2 * n_tok] + part[2 * n_tok:]

    def loop(body):
        def step(c, carry):
            body(c)
            return carry
        lax.fori_loop(0, n_chunk, step, 0)

    expert_up(0)
    loop(lambda c: expert_down(0, c))
    expert_up(1)
    for l in range(n_loc):
        for h in range(n_half):
            for m, dc in PEERS:
                spread_copy(l, h, m, dc).wait_send()

    def down_and_forward(c):
        expert_down(1, c)
        forward(0, c)

    loop(down_and_forward)

    def forward_and_collect(c):
        forward(1, c)
        collect(0, c)

    loop(forward_and_collect)

    def finish(c):
        collect(1, c)
        out_ref[:, cols_at(c)] = acc[:, cols_at(c)].astype(BF16)

    loop(finish)

    for m in MATES:
        mt_copy(m).wait_send()
        for h in range(n_half):
            gather_copy(m, h).wait_send()

    def drain(c):
        for l in range(n_loc):
            for copy in back_copies(l, c):
                copy.wait_send()
            for m in MATES:
                home_copy(l, c, m).wait_send()

    loop(drain)


def solution(mesh):
    group_axes = ('ep2', 'ep')
    n_line = mesh.shape['ep2']
    n_group = n_line * mesh.shape['ep']
    row_spec = P(('dp', 'ep2', 'ep'), None)
    weight_spec = P(group_axes, None, None)

    def device_step(tokens, expert_ids, gates, w_gate, w_up, w_down):
        n_tok, n_top = expert_ids.shape
        n_loc, dim, ffn = w_gate.shape
        n_exp = n_loc * n_group
        cap = -(-(n_tok * n_top) // n_exp)
        n_rows = n_group * cap
        n_half, n_chunk, f_tile, n_w2 = 2, 5, 256, 4
        sem = pltpu.SemaphoreType.DMA
        vmem = pl.BlockSpec(memory_space=pltpu.VMEM)
        hbm = pl.BlockSpec(memory_space=pl.ANY)
        n_dev = 2 * n_line
        return pl.pallas_call(
            functools.partial(moe_kernel, n_line, cap, n_half, n_chunk, f_tile),
            out_shape=jax.ShapeDtypeStruct((n_tok, dim), BF16),
            in_specs=[vmem, vmem, vmem, hbm, hbm, hbm],
            out_specs=vmem,
            scratch_shapes=[
                pltpu.VMEM((n_loc, dim, ffn), BF16),
                pltpu.VMEM((n_loc, dim, ffn), BF16),
                pltpu.VMEM((n_w2, ffn, dim // n_chunk), BF16),
                pltpu.VMEM((n_line, n_exp, n_tok), BF16),
                pltpu.VMEM((n_tok, n_exp), BF16),
                pltpu.VMEM((n_line * n_tok, dim), BF16),
                pltpu.VMEM((n_loc, n_rows, n_line * n_tok), BF16),
                pltpu.VMEM((n_loc, n_rows, dim), BF16),
                pltpu.VMEM((n_loc, n_rows, dim), BF16),
                pltpu.VMEM((n_rows, ffn), BF16),
                pltpu.VMEM((n_loc, n_rows, dim), BF16),
                pltpu.VMEM((n_loc, n_rows, dim), BF16),
                pltpu.VMEM((n_rows, n_rows), BF16),
                pltpu.VMEM((n_loc, 3 * n_tok, n_rows), BF16),
                pltpu.VMEM((n_tok, dim), F32),
                sem((2, n_loc)),
                sem((n_w2,)),
                sem((n_line - 1,)), sem((n_line - 1,)),
                sem((n_line - 1, n_half)), sem((n_line - 1, n_half)),
                sem((n_loc, n_half, n_dev)), sem((n_loc, n_half, n_dev)),
                sem((n_loc, n_chunk, n_dev)), sem((n_loc, n_chunk, n_dev)),
                sem((n_loc, n_chunk, n_line - 1)), sem((n_loc, n_chunk, n_line - 1)),
            ],
            compiler_params=pltpu.CompilerParams(
                collective_id=0, has_side_effects=True, vmem_limit_bytes=67043328),
        )(tokens, expert_ids, gates, w_gate, w_up, w_down)

    return jax.shard_map(
        device_step, mesh=mesh,
        in_specs=(row_spec, row_spec, row_spec, weight_spec, weight_spec, weight_spec),
        out_specs=row_spec, check_vma=False)
```

time: 168 us -> 103 us (0.61)
  Pallas kernels: 0 us -> 97.3 us
  blocking collectives: 58.9 us -> 0 us
  waiting for transfers between devices: 51.5 us -> 0 us
  matrix products: 36.2 us -> 0 us
  local copies, waits for them, and re-layouts: 10.7 us -> 4.8 us
  starting transfers between devices: 5.01 us -> 0 us
  other arithmetic: 4.62 us -> 0 us
    pallas_call x0 -> x1, Pallas kernels: none -> 97.3 us  [device_step(): pl.pallas_call(functools.partial(moe_kernel, n_line, cap, n_half, n_chunk...]
    all_to_all x1 -> x0, blocking collectives: 58.9 us -> none  [device_step(): recv_buf = lax.all_to_all(send_buf, group_axes, 0, 0, tiled=True)]
    all_to_all x1 -> x0, waiting for transfers between devices: 51.5 us -> none  [device_step(): lax.all_to_all(expert_out.reshape(n_expert * row_cap, model_dim), group_a...]
    dot_general x4 -> x0, matrix products: 36.2 us -> none  [the longest x1 20.6 us: expert_ffn(): jnp.einsum('slcf,lfd->slcd', hidden, w_down, preferred_element_type=jnp.f...]
    all_to_all x2 -> x0, local copies, waits for them, and re-layouts: 7.3 us -> none  [the longest x1 6.14 us: device_step(): lax.all_to_all(expert_out.reshape(n_expert * row_cap, model_dim), group_a...]
    all_to_all x1 -> x0, starting transfers between devices: 5.01 us -> none  [device_step(): lax.all_to_all(expert_out.reshape(n_expert * row_cap, model_dim), group_a...]
    unnamed x9 -> x3, local copies, waits for them, and re-layouts: 2.68 us -> 4.8 us
    another operation x2 -> x0, other arithmetic: 1.82 us -> none
  transfers between devices with their start and end apart: 1 -> 0, of which waited for: 1 -> 0; matrix products, arithmetic and copies ran while one was open for 0% -> 0% of each run, Pallas kernels for 0% -> 0%
where the time goes in v1:
time: 103 us; the launch traced here: 102 us
  Pallas kernels  97.3 us (94%)
  local copies, waits for them, and re-layouts  4.8 us (5%)
    pallas_call x1, Pallas kernels, device_step(): pl.pallas_call(functools.partial(moe_kernel, n_line, cap, n_half, n_chunk...  97.3 us
    unnamed x3, local copies, waits for them, and re-layouts  4.8 us

profile of v1, /device:TPU:97, one launch (start us, length us, event | category | flops | bytes accessed | tf_op | source)
XLA Modules:
  0.0 102.2 jit_solution(11351567665625910159)
XLA Ops:
  0.0 1.4 %copy.7.idx_ref = s32[128,6]{1,0:T(8,128)} copy(s32[128,6]{0,1:T(8,128)} %param.7) | data formatting | bytes 6144 | tf_op args[1]
  1.4 1.4 %copy.8.gate_ref = f32[128,6]{1,0:T(8,128)} copy(f32[128,6]{0,1:T(8,128)} %param.8) | data formatting | bytes 6144 | tf_op args[2]
  2.8 97.3 %shard_map.64 = bf16[128,2560]{1,0:T(8,128)(2,1)} custom-call(bf16[128,2560]{1,0:T(8,128)(2,1)} %x_ref.1, s32[128,6]{1,0:T(8,128)} %copy.7.idx_ref, f32[128,6]{1,0:T(8,128)} %copy.8.gate_ref, bf16[2,2560,1536]{2,1,0:T(8,128)(2,1)} %w1_hbm.1, bf16[2,2560,1536]{2,1,0:T(8,128)(2,1)} %w3_hbm.1, bf16[2,1536,2560]{2,1,0:T(8,128)(2,1)} %w2_hbm.1), custom_call_target="tpu_custom_call" | custom-call | tf_op jit(solution)/shard_map/pallas_call | solution.py:350
  100.2 2.0 %copy.10 = bf16[128,2560]{1,0:T(8,128)(2,1)} copy(bf16[128,2560]{1,0:T(8,128)(2,1)} %shard_map.64) | data formatting | bytes 1310720

commit v2 on v1

v2 whole, which is shorter than its diff:
```python
import functools

import jax
import jax.numpy as jnp
from jax import lax
from jax.experimental import pallas as pl
from jax.experimental.pallas import tpu as pltpu
from jax.sharding import PartitionSpec as P

MESH = pl.DeviceIdType.MESH
F32 = jnp.float32
BF16 = jnp.bfloat16
PEERS = [(1, 0), (3, 0), (1, 1), (3, 1), (2, 0), (2, 1), (0, 1)]
MATES = [1, 3, 2]


def div12(v):
    return (v * 2731) >> 15


def nt_dot(a, b):
    return lax.dot_general(a, b, (((1,), (1,)), ((), ())), preferred_element_type=F32)


def dot(a, b):
    return jnp.dot(a, b, preferred_element_type=F32)


def moe_kernel(
    n_line, cap, n_half, n_chunk, f_tile, cuts, ahead, lead,
    x_hbm, idx_hbm, gate_hbm, w1_hbm, w3_hbm, w2_hbm, out_ref,
    x_ref, idx_ref, gate_ref, w1, w3, w2, mts, xg, sel, sendb, rows, part_a, part_b, hid, y1, y3, perm, gmat, acc,
    in_sem, w13_sem, w2_sem, mt_s, mt_r, g_s, g_r, d_s, d_r, c_s, c_r, e_s, e_r,
):
    n_tok, dim = x_ref.shape
    n_top = idx_ref.shape[0]
    n_loc, ffn = w2_hbm.shape[0], w2_hbm.shape[1]
    n_exp = mts.shape[1]
    per = n_line * cap
    n_rows = 2 * n_line * per
    n_w2 = w2.shape[0]
    half = dim // n_half
    wide = dim // n_chunk

    dp = lax.axis_index('dp')
    yy = lax.axis_index('ep2')
    ee = lax.axis_index('ep')
    xx = ee // 2
    cc = lax.rem(ee, 2)
    k_self = jnp.where(cc == 0, yy, xx)
    q_self = jnp.where(cc == 0, xx, yy)
    i_self = cc * n_line + q_self
    d_self = 2 * q_self + cc
    coef_k = jnp.where(cc == 0, 16, 4)
    coef_q = jnp.where(cc == 0, 4, 16)

    def mod(v):
        return lax.rem(v + n_line, n_line)

    def mate(m):
        k = mod(k_self + m)
        return (dp, jnp.where(cc == 0, k, yy), jnp.where(cc == 0, xx, k) * 2 + cc)

    def spread_peer(m, dc):
        q = mod(q_self + m)
        c2 = lax.rem(cc + dc, 2)
        dev = (dp, jnp.where(cc == 0, yy, q), jnp.where(cc == 0, q, xx) * 2 + c2)
        return dev, 2 * q + c2

    def rows_at(start, size, unit):
        return pl.ds(pl.multiple_of(start, unit), size)

    def half_cols(h):
        return pl.ds(h * half, half)

    def cols_at(c):
        return pl.ds(pl.multiple_of(c * wide, wide), wide)

    def w13_copy(which, l):
        hbm, buf = ((w1_hbm, w1), (w3_hbm, w3))[which]
        return pltpu.make_async_copy(hbm.at[l], buf.at[l], w13_sem.at[which, l])

    def w2_copy(t):
        slot = lax.rem(t, n_w2)
        return pltpu.make_async_copy(
            w2_hbm.at[t // n_chunk, :, cols_at(lax.rem(t, n_chunk))], w2.at[slot], w2_sem.at[slot])

    def mt_copy(m):
        return pltpu.make_async_remote_copy(
            mts.at[k_self], mts.at[k_self], mt_s.at[0], mt_r.at[0], device_id=mate(m), device_id_type=MESH)

    def gather_copy(m, h):
        return pltpu.make_async_remote_copy(
            x_ref.at[:, half_cols(h)], xg.at[rows_at(k_self * n_tok, n_tok, 8), half_cols(h)],
            g_s.at[0], g_r.at[m // 2, h], device_id=mate(m), device_id_type=MESH)

    def relay_copy(m, h):
        side = m // 2
        block = xg.at[rows_at(mod(k_self - m) * n_tok + side * (n_tok // 2), n_tok // 2, 8), half_cols(h)]
        return pltpu.make_async_remote_copy(
            block, block, g_s.at[0], g_r.at[2 + side, h], device_id=mate(m), device_id_type=MESH)

    def wait_bytes(ref, sem):
        pltpu.make_async_copy(ref, ref, sem).wait()

    def spread_copy(l, h, m, dc):
        dev, d = spread_peer(m, dc)
        return pltpu.make_async_remote_copy(
            sendb.at[l, rows_at(d * per, per, 8), half_cols(h)],
            rows.at[l, rows_at(i_self * per, per, 8), half_cols(h)],
            d_s.at[0], d_r.at[l, h], device_id=dev, device_id_type=MESH)

    others = (2 * n_line - 1) * per

    def spread_wait(l, h):
        wait_bytes(rows.at[l, pl.ds(0, others), half_cols(h)], d_r.at[l, h])

    def back_targets():
        out = []
        for m in (1, 3, 2):
            for side in (0, 1):
                pos = mod((yy if side else xx) + m)
                dev = (dp, pos, xx * 2 + 1) if side else (dp, yy, pos * 2)
                d_me = 2 * (yy if side else xx) + cc
                out.append((side * n_line + pos, dev, d_me))
        other = 1 - cc
        pos = jnp.where(other == 0, xx, yy)
        out.append((other * n_line + pos, (dp, yy, xx * 2 + other), 2 * pos + cc))
        return out

    def back_copies(l, c):
        return [
            pltpu.make_async_remote_copy(
                rows.at[l, rows_at(i * per, per, 8), cols_at(c)], y1.at[l, rows_at(d_me * per, per, 8), cols_at(c)],
                c_s.at[0], c_r.at[l, c], device_id=dev, device_id_type=MESH)
            for i, dev, d_me in back_targets()
        ]

    def back_wait(l, c):
        wait_bytes(y1.at[l, pl.ds(0, others), cols_at(c)], c_r.at[l, c])

    home = 2 * n_line * cap

    def home_copy(l, c, m):
        s = mod(k_self + m)
        return pltpu.make_async_remote_copy(
            sendb.at[l, rows_at(s * home, home, 8), cols_at(c)], y3.at[l, rows_at(k_self * home, home, 8), cols_at(c)],
            e_s.at[0], e_r.at[l, c], device_id=mate(m), device_id_type=MESH)

    inputs = [
        pltpu.make_async_copy(src, dst, in_sem.at[n])
        for n, (src, dst) in enumerate(((idx_hbm, idx_ref), (x_hbm, x_ref), (gate_hbm, gate_ref)))
    ]
    for copy in inputs:
        copy.start()

    barrier = pltpu.get_barrier_semaphore()
    for side in (0, 1):
        for m in range(n_line):
            for dc in (0, 1):
                if (m, dc) == (0, 0) or (side and m == 0):
                    continue
                pos = mod((yy if side else xx) + m)
                c2 = lax.rem(cc + dc, 2)
                dev = (dp, pos, xx * 2 + c2) if side else (dp, yy, pos * 2 + c2)
                pl.semaphore_signal(barrier, inc=1, device_id=dev, device_id_type=MESH)

    for l in range(n_loc):
        for which in range(2):
            w13_copy(which, l).start()
    for t in range(n_w2):
        w2_copy(t).start()

    row_e = lax.broadcasted_iota(jnp.int32, (n_exp, n_tok), 0)
    inputs[0].wait()
    chosen = jnp.zeros((n_exp, n_tok), F32)
    for j in range(n_top):
        chosen = chosen + (idx_ref[j:j + 1, :] == row_e).astype(F32)
    before = (lax.broadcasted_iota(jnp.int32, (n_tok, n_tok), 0)
              < lax.broadcasted_iota(jnp.int32, (n_tok, n_tok), 1)).astype(BF16)
    slot = dot(chosen.astype(BF16), before)
    slot = jnp.where(chosen > 0, slot, -1.0).astype(BF16)
    mts[k_self] = slot

    with jax.named_scope('entry_wait'):
        pl.semaphore_wait(barrier, 4 * n_line - 3)

    inputs[1].wait()
    inputs[2].wait()
    for m in MATES:
        mt_copy(m).start()
    for h in range(ahead):
        for m in (1, 3):
            gather_copy(m, h).start()

    xg[rows_at(k_self * n_tok, n_tok, 8), :] = x_ref[...]

    r = lax.broadcasted_iota(jnp.int32, (n_rows, 1), 0)
    r12 = div12(r)
    r_slot = (r - r12 * cap).astype(F32)
    r_src = r12 & (n_line - 1)
    r_dev = r12 >> 2
    r_exp0 = coef_k * k_self + coef_q * (r_dev >> 1) + 2 * (r_dev & 1)
    e_lane = lax.broadcasted_iota(jnp.int32, (n_rows, n_exp), 1)
    with jax.named_scope('slots_wait'):
        wait_bytes(mts.at[pl.ds(0, n_line - 1)], mt_r.at[0])
    for l in range(n_loc):
        pick = (e_lane == r_exp0 + l).astype(BF16)
        for s in range(n_line):
            val = dot(pick, mts[s])
            hit = jnp.logical_and(val == r_slot, r_src == s)
            sel[l, :, s * n_tok:(s + 1) * n_tok] = jnp.where(hit, 1.0, 0.0).astype(BF16)

    def spread(l, h):
        sendb[l, :, half_cols(h)] = dot(sel[l], xg[:, half_cols(h)]).astype(BF16)
        for m, dc in PEERS:
            spread_copy(l, h, m, dc).start()
        rows[l, rows_at(i_self * per, per, 8), half_cols(h)] = sendb[l, rows_at(d_self * per, per, 8), half_cols(h)]

    def relay(h):
        for m in (1, 3):
            gather_copy(m, h).wait_recv()
            relay_copy(m, h).start()

    with jax.named_scope('gather_and_spread'):
        for h in range(lead):
            relay(h)
        for h in range(n_half):
            with jax.named_scope('gather_wait'):
                if h + lead < n_half:
                    relay(h + lead)
                if h + ahead < n_half:
                    for m in (1, 3):
                        gather_copy(m, h + ahead).start()
                for m in (1, 3):
                    relay_copy(m, h).wait_recv()
            with jax.named_scope('spread_send'):
                spread(0, h)
    with jax.named_scope('spread_rest'):
        for h in range(n_half):
            for l in range(1, n_loc):
                spread(l, h)

    o12 = r12
    o_in = (o12 & 7) * per + (o12 >> 3) * cap + (r - r12 * cap)
    perm[...] = (lax.broadcasted_iota(jnp.int32, (n_rows, n_rows), 1) == o_in).astype(BF16)

    gate = jnp.zeros((n_exp, n_tok), F32)
    for j in range(n_top):
        gate = gate + jnp.where(idx_ref[j:j + 1, :] == row_e, gate_ref[j:j + 1, :], 0.0)
    eye = (lax.broadcasted_iota(jnp.int32, (n_tok, n_tok), 0)
           == lax.broadcasted_iota(jnp.int32, (n_tok, n_tok), 1)).astype(BF16)
    slot_t = nt_dot(eye, mts[k_self]).astype(BF16)
    parts = []
    rest = gate
    for _ in range(3):
        part = rest.astype(BF16)
        parts.append(nt_dot(eye, part).astype(BF16))
        rest = rest - part.astype(F32)
    q = lax.broadcasted_iota(jnp.int32, (1, n_rows), 1)
    q12 = div12(q)
    q_slot = (q - q12 * cap).astype(F32)
    q_dev = q12 & 7
    q_exp0 = coef_k * (q12 >> 3) + coef_q * (q_dev >> 1) + 2 * (q_dev & 1)
    e_row = lax.broadcasted_iota(jnp.int32, (n_exp, n_rows), 0)
    for l in range(n_loc):
        spread_e = (e_row == q_exp0 + l).astype(BF16)
        hit = dot(slot_t, spread_e) == q_slot
        for p in range(3):
            gmat[l, p * n_tok:(p + 1) * n_tok, :] = jnp.where(hit, dot(parts[p], spread_e), 0.0).astype(BF16)
    acc[...] = x_ref[...].astype(F32)

    def expert_up(l, cuts):
        with jax.named_scope('weight_wait'):
            for which in range(2):
                w13_copy(which, l).wait()
        edges = (0,) + cuts + (n_half,)
        for h0, h1 in zip(edges, edges[1:]):
            with jax.named_scope('spread_wait'):
                for h in range(h0, h1):
                    spread_wait(l, h)
            k = slice(h0 * half, h1 * half)

            def tile(n, carry, h0=h0, h1=h1, k=k):
                cols = pl.ds(pl.multiple_of(n * f_tile, f_tile), f_tile)
                a = dot(rows[l, :, k], w1[l, k, cols])
                b = dot(rows[l, :, k], w3[l, k, cols])
                if h0 > 0:
                    a = a + part_a[:, cols]
                    b = b + part_b[:, cols]
                if h1 < n_half:
                    part_a[:, cols] = a
                    part_b[:, cols] = b
                else:
                    hid[:, cols] = (jax.nn.silu(a) * b).astype(BF16)
                return carry

            with jax.named_scope('up'):
                lax.fori_loop(0, ffn // f_tile, tile, 0)

    def expert_down(l, c):
        t = l * n_chunk + c
        w2_copy(t).wait()
        rows[l, :, cols_at(c)] = dot(hid[...], w2[lax.rem(t, n_w2)]).astype(BF16)

        @pl.when(t + n_w2 < n_loc * n_chunk)
        def _():
            w2_copy(t + n_w2).start()

        for copy in back_copies(l, c):
            copy.start()
        y1[l, rows_at(d_self * per, per, 8), cols_at(c)] = rows[l, rows_at(i_self * per, per, 8), cols_at(c)]

    def forward(l, c):
        with jax.named_scope('back_wait'):
            back_wait(l, c)
        sendb[l, :, cols_at(c)] = dot(perm[...], y1[l, :, cols_at(c)]).astype(BF16)
        for m in MATES:
            home_copy(l, c, m).start()
        y3[l, rows_at(k_self * home, home, 8), cols_at(c)] = sendb[l, rows_at(k_self * home, home, 8), cols_at(c)]

    def collect(l, c):
        with jax.named_scope('home_wait'):
            wait_bytes(y3.at[l, pl.ds(0, (n_line - 1) * home), cols_at(c)], e_r.at[l, c])
        part = dot(gmat[l], y3[l, :, cols_at(c)])
        acc[:, cols_at(c)] += part[:n_tok] + part[n_tok:2 * n_tok] + part[2 * n_tok:]

    def loop(body):
        def step(c, carry):
            body(c)
            return carry
        lax.fori_loop(0, n_chunk, step, 0)

    expert_up(0, cuts[0])
    with jax.named_scope('down0'):
        loop(lambda c: expert_down(0, c))
    expert_up(1, cuts[1])
    with jax.named_scope('spread_drain'):
        wait_bytes(sendb.at[:, pl.ds(0, others), :], d_s.at[0])

    def down_and_forward(c):
        expert_down(1, c)
        forward(0, c)

    with jax.named_scope('down1_forward0'):
        loop(down_and_forward)

    def forward_and_collect(c):
        forward(1, c)
        collect(0, c)

    with jax.named_scope('forward1_collect0'):
        loop(forward_and_collect)

    def finish(c):
        collect(1, c)
        out_ref[:, cols_at(c)] = acc[:, cols_at(c)].astype(BF16)

    with jax.named_scope('collect1'):
        loop(finish)

    with jax.named_scope('drain'):
        wait_bytes(mts.at[pl.ds(0, n_line - 1)], mt_s.at[0])
        wait_bytes(xg.at[pl.ds(0, (n_line - 1) * n_tok), :], g_s.at[0])
        wait_bytes(y1.at[:, pl.ds(0, others), :], c_s.at[0])
        wait_bytes(y3.at[:, pl.ds(0, (n_line - 1) * home), :], e_s.at[0])


def solution(mesh):
    group_axes = ('ep2', 'ep')
    n_line = mesh.shape['ep2']
    n_group = n_line * mesh.shape['ep']
    row_spec = P(('dp', 'ep2', 'ep'), None)
    weight_spec = P(group_axes, None, None)

    def device_step(tokens, expert_ids, gates, w_gate, w_up, w_down):
        n_tok, n_top = expert_ids.shape
        n_loc, dim, ffn = w_gate.shape
        n_exp = n_loc * n_group
        cap = -(-(n_tok * n_top) // n_exp)
        n_rows = n_group * cap
        n_half, n_chunk, f_tile, n_w2, cuts, ahead, lead = 5, 5, 256, 3, ((2, 4), (2, 4)), 5, 5
        sem = pltpu.SemaphoreType.DMA
        vmem = pl.BlockSpec(memory_space=pltpu.VMEM)
        hbm = pl.BlockSpec(memory_space=pl.ANY)
        n_dev = 2 * n_line
        return pl.pallas_call(
            functools.partial(moe_kernel, n_line, cap, n_half, n_chunk, f_tile, cuts, ahead, lead),
            out_shape=jax.ShapeDtypeStruct((n_tok, dim), BF16),
            in_specs=[hbm] * 6,
            out_specs=vmem,
            scratch_shapes=[
                pltpu.VMEM((n_tok, dim), BF16),
                pltpu.VMEM((n_top, n_tok), jnp.int32),
                pltpu.VMEM((n_top, n_tok), F32),
                pltpu.VMEM((n_loc, dim, ffn), BF16),
                pltpu.VMEM((n_loc, dim, ffn), BF16),
                pltpu.VMEM((n_w2, ffn, dim // n_chunk), BF16),
                pltpu.VMEM((n_line, n_exp, n_tok), BF16),
                pltpu.VMEM((n_line * n_tok, dim), BF16),
                pltpu.VMEM((n_loc, n_rows, n_line * n_tok), BF16),
                pltpu.VMEM((n_loc, n_rows, dim), BF16),
                pltpu.VMEM((n_loc, n_rows, dim), BF16),
                pltpu.VMEM((n_rows, ffn), F32),
                pltpu.VMEM((n_rows, ffn), F32),
                pltpu.VMEM((n_rows, ffn), BF16),
                pltpu.VMEM((n_loc, n_rows, dim), BF16),
                pltpu.VMEM((n_loc, n_rows, dim), BF16),
                pltpu.VMEM((n_rows, n_rows), BF16),
                pltpu.VMEM((n_loc, 3 * n_tok, n_rows), BF16),
                pltpu.VMEM((n_tok, dim), F32),
                sem((3,)),
                sem((2, n_loc)),
                sem((n_w2,)),
                sem((1,)), sem((1,)),
                sem((1,)), sem((4, n_half)),
                sem((1,)), sem((n_loc, n_half)),
                sem((1,)), sem((n_loc, n_chunk)),
                sem((1,)), sem((n_loc, n_chunk)),
            ],
            compiler_params=pltpu.CompilerParams(
                collective_id=0, has_side_effects=True, vmem_limit_bytes=67043328),
        )(tokens, expert_ids.T, gates.T, w_gate, w_up, w_down)

    return jax.shard_map(
        device_step, mesh=mesh,
        in_specs=(row_spec, row_spec, row_spec, weight_spec, weight_spec, weight_spec),
        out_specs=row_spec, check_vma=False)
```

time: 103 us -> 88.9 us (0.86)
  Pallas kernels: 97.3 us -> 86.8 us
  local copies, waits for them, and re-layouts: 4.8 us -> 1.97 us
    pallas_call x1, Pallas kernels: 97.3 us -> 86.8 us  [device_step(): pl.pallas_call(functools.partial(moe_kernel, n_line, cap, n_half, n_chunk...]
    unnamed x3 -> x1, local copies, waits for them, and re-layouts: 4.8 us -> 1.97 us
where the time goes in v2:
time: 88.9 us; the launch traced here: 88.8 us
  Pallas kernels  86.8 us (98%)
  local copies, waits for them, and re-layouts  1.97 us (2%)
    pallas_call x1, Pallas kernels, device_step(): pl.pallas_call(functools.partial(moe_kernel, n_line, cap, n_half, n_chunk...  86.8 us
    unnamed x1, local copies, waits for them, and re-layouts  1.97 us

profile of v2, /device:TPU:97, one launch (start us, length us, event | category | flops | bytes accessed | tf_op | source)
XLA Modules:
  0.0 88.8 jit_solution(8958083738163166136)
XLA Ops:
  0.0 86.8 %shard_map.64 = bf16[128,2560]{1,0:T(8,128)(2,1)} custom-call(bf16[128,2560]{1,0:T(8,128)(2,1)} %x_hbm.1, s32[6,128]{1,0:T(8,128)} %bitcast.2, f32[6,128]{1,0:T(8,128)} %bitcast.3, bf16[2,2560,1536]{2,1,0:T(8,128)(2,1)} %w1_hbm.1, bf16[2,2560,1536]{2,1,0:T(8,128)(2,1)} %w3_hbm.1, bf16[2,1536,2560]{2,1,0:T(8,128)(2,1)} %w2_hbm.1), custom_call_target="tpu_custom_call" | custom-call | tf_op jit(solution)/shard_map/pallas_call | solution.py:387
  86.9 2.0 %copy.8 = bf16[128,2560]{1,0:T(8,128)(2,1)} copy(bf16[128,2560]{1,0:T(8,128)(2,1)} %shard_map.64) | data formatting | bytes 1310720

commit v3 on v2

--- a/solution.py
+++ b/solution.py
@@ -27,15 +27,17 @@
 
 
 def moe_kernel(
-    n_line, cap, n_half, n_chunk, f_tile, cuts, ahead, lead,
-    x_hbm, idx_hbm, gate_hbm, w1_hbm, w3_hbm, w2_hbm, out_ref,
-    x_ref, idx_ref, gate_ref, w1, w3, w2, mts, xg, sel, sendb, rows, part_a, part_b, hid, y1, y3, perm, gmat, acc,
-    in_sem, w13_sem, w2_sem, mt_s, mt_r, g_s, g_r, d_s, d_r, c_s, c_r, e_s, e_r,
+    n_line, cap, n_half, n_chunk, f_tile, cuts, ahead, lag,
+    x_hbm, idx_hbm, gate_hbm, w1_hbm, w3_hbm, w2_hbm, out_hbm,
+    x_ref, idx_ref, gate_ref, w1, w3, w2, slots, gates, mts, slots_far, gates_near, xg, sel, sendb, rows, part_a, part_b, hid, y1,
+    y_raw, y_far, perm, gmat, acc, part_out, part_in,
+    in_sem, out_sem, w13_sem, w2_sem, mt_s, mt_r, n_s, n_r, g_s, g_r, d_s, d_r, c_s, c_r, e_s, e_r, f_r, p_s, p_r,
 ):
     n_tok, dim = x_ref.shape
     n_top = idx_ref.shape[0]
     n_loc, ffn = w2_hbm.shape[0], w2_hbm.shape[1]
-    n_exp = mts.shape[1]
+    n_exp = slots.shape[0]
+    n_line_exp = n_exp // n_line
     per = n_line * cap
     n_rows = 2 * n_line * per
     n_w2 = w2.shape[0]
@@ -87,7 +89,7 @@
 
     def mt_copy(m):
         return pltpu.make_async_remote_copy(
-            mts.at[k_self], mts.at[k_self], mt_s.at[0], mt_r.at[0], device_id=mate(m), device_id_type=MESH)
+            slots.at[line_rows(mod(k_self + m)), :], mts.at[k_self], mt_s.at[0], mt_r.at[0], device_id=mate(m), device_id_type=MESH)
 
     def gather_copy(m, h):
         return pltpu.make_async_remote_copy(
@@ -140,12 +142,46 @@
         wait_bytes(y1.at[l, pl.ds(0, others), cols_at(c)], c_r.at[l, c])
 
     home = 2 * n_line * cap
-
-    def home_copy(l, c, m):
-        s = mod(k_self + m)
-        return pltpu.make_async_remote_copy(
-            sendb.at[l, rows_at(s * home, home, 8), cols_at(c)], y3.at[l, rows_at(k_self * home, home, 8), cols_at(c)],
-            e_s.at[0], e_r.at[l, c], device_id=mate(m), device_id_type=MESH)
+    both = n_loc * home
+
+    def at_home(s, l):
+        return s >> 1, rows_at((s & 1) * both + l * home, home, 8)
+
+    def side_cols(c, side):
+        return pl.ds(pl.multiple_of(c * wide + side * (wide // 2), wide // 2), wide // 2)
+
+    def raw_copy(l, c, m):
+        side = m // 2
+        p, r = at_home(mod(k_self + m), l)
+        return pltpu.make_async_remote_copy(
+            sendb.at[p, r, side_cols(c, side)], y_raw.at[pl.ds(l * home, home), side_cols(c, side)],
+            e_s.at[0], e_r.at[c], device_id=mate(m), device_id_type=MESH)
+
+    def far_copy(l, c, m):
+        side = 1 - m // 2
+        p, r = at_home(mod(k_self + 2), l)
+        return pltpu.make_async_remote_copy(
+            sendb.at[p, r, side_cols(c, side)], y_far.at[pl.ds(l * home, home), side_cols(c, side)],
+            e_s.at[0], f_r.at[c], device_id=mate(m), device_id_type=MESH)
+
+    def sum_copy(c, m):
+        cols = side_cols(c, 1 - m // 2)
+        return pltpu.make_async_remote_copy(
+            part_out.at[:, cols], part_in.at[:, cols], p_s.at[0], p_r.at[c], device_id=mate(m), device_id_type=MESH)
+
+    def line_rows(k):
+        return pl.ds(pl.multiple_of(k * n_line_exp, n_line_exp), n_line_exp)
+
+    def note_copies(m):
+        side = m // 2
+        out = [pltpu.make_async_remote_copy(
+            slots.at[line_rows(mod(k_self + 2)), :], slots_far.at[side], n_s.at[0], n_r.at[0],
+            device_id=mate(m), device_id_type=MESH)]
+        for n, k in enumerate((mod(k_self + m), mod(k_self + 2))):
+            out.append(pltpu.make_async_remote_copy(
+                gates.at[line_rows(k), :], gates_near.at[side, n], n_s.at[1], n_r.at[1],
+                device_id=mate(m), device_id_type=MESH))
+        return out
 
     inputs = [
         pltpu.make_async_copy(src, dst, in_sem.at[n])
@@ -171,7 +207,8 @@
     for t in range(n_w2):
         w2_copy(t).start()
 
-    row_e = lax.broadcasted_iota(jnp.int32, (n_exp, n_tok), 0)
+    r_e = lax.broadcasted_iota(jnp.int32, (n_exp, n_tok), 0)
+    row_e = (coef_k * (r_e >> 4) + coef_q * ((r_e >> 2) & 3) + (r_e & 3))
     inputs[0].wait()
     chosen = jnp.zeros((n_exp, n_tok), F32)
     for j in range(n_top):
@@ -180,13 +217,19 @@
               < lax.broadcasted_iota(jnp.int32, (n_tok, n_tok), 1)).astype(BF16)
     slot = dot(chosen.astype(BF16), before)
     slot = jnp.where(chosen > 0, slot, -1.0).astype(BF16)
-    mts[k_self] = slot
+    slots[...] = slot
+    mts[k_self] = slots[line_rows(k_self), :]
+
+    inputs[2].wait()
+    gate = jnp.zeros((n_exp, n_tok), F32)
+    for j in range(n_top):
+        gate = gate + jnp.where(idx_ref[j:j + 1, :] == row_e, gate_ref[j:j + 1, :], 0.0)
+    gates[...] = gate
 
     with jax.named_scope('entry_wait'):
         pl.semaphore_wait(barrier, 4 * n_line - 3)
 
     inputs[1].wait()
-    inputs[2].wait()
     for m in MATES:
         mt_copy(m).start()
     for h in range(ahead):
@@ -200,12 +243,11 @@
     r_slot = (r - r12 * cap).astype(F32)
     r_src = r12 & (n_line - 1)
     r_dev = r12 >> 2
-    r_exp0 = coef_k * k_self + coef_q * (r_dev >> 1) + 2 * (r_dev & 1)
-    e_lane = lax.broadcasted_iota(jnp.int32, (n_rows, n_exp), 1)
+    e_lane = lax.broadcasted_iota(jnp.int32, (n_rows, n_line_exp), 1)
     with jax.named_scope('slots_wait'):
         wait_bytes(mts.at[pl.ds(0, n_line - 1)], mt_r.at[0])
     for l in range(n_loc):
-        pick = (e_lane == r_exp0 + l).astype(BF16)
+        pick = (e_lane == n_loc * r_dev + l).astype(BF16)
         for s in range(n_line):
             val = dot(pick, mts[s])
             hit = jnp.logical_and(val == r_slot, r_src == s)
@@ -223,15 +265,16 @@
             relay_copy(m, h).start()
 
     with jax.named_scope('gather_and_spread'):
-        for h in range(lead):
+        for h in range(n_half):
             relay(h)
+            if h + ahead < n_half:
+                for m in (1, 3):
+                    gather_copy(m, h + ahead).start()
+        for m in (1, 3):
+            for copy in note_copies(m):
+                copy.start()
         for h in range(n_half):
             with jax.named_scope('gather_wait'):
-                if h + lead < n_half:
-                    relay(h + lead)
-                if h + ahead < n_half:
-                    for m in (1, 3):
-                        gather_copy(m, h + ahead).start()
                 for m in (1, 3):
                     relay_copy(m, h).wait_recv()
             with jax.named_scope('spread_send'):
@@ -245,29 +288,39 @@
     o_in = (o12 & 7) * per + (o12 >> 3) * cap + (r - r12 * cap)
     perm[...] = (lax.broadcasted_iota(jnp.int32, (n_rows, n_rows), 1) == o_in).astype(BF16)
 
-    gate = jnp.zeros((n_exp, n_tok), F32)
-    for j in range(n_top):
-        gate = gate + jnp.where(idx_ref[j:j + 1, :] == row_e, gate_ref[j:j + 1, :], 0.0)
     eye = (lax.broadcasted_iota(jnp.int32, (n_tok, n_tok), 0)
            == lax.broadcasted_iota(jnp.int32, (n_tok, n_tok), 1)).astype(BF16)
-    slot_t = nt_dot(eye, mts[k_self]).astype(BF16)
-    parts = []
-    rest = gate
-    for _ in range(3):
-        part = rest.astype(BF16)
-        parts.append(nt_dot(eye, part).astype(BF16))
-        rest = rest - part.astype(F32)
-    q = lax.broadcasted_iota(jnp.int32, (1, n_rows), 1)
+    q = lax.broadcasted_iota(jnp.int32, (1, both), 1)
     q12 = div12(q)
     q_slot = (q - q12 * cap).astype(F32)
-    q_dev = q12 & 7
-    q_exp0 = coef_k * (q12 >> 3) + coef_q * (q_dev >> 1) + 2 * (q_dev & 1)
-    e_row = lax.broadcasted_iota(jnp.int32, (n_exp, n_rows), 0)
-    for l in range(n_loc):
-        spread_e = (e_row == q_exp0 + l).astype(BF16)
-        hit = dot(slot_t, spread_e) == q_slot
+    q_exp = n_loc * (q12 & 7) + (q12 >> 3)
+    spread_e = (lax.broadcasted_iota(jnp.int32, (n_line_exp, both), 0) == q_exp).astype(BF16)
+
+    def gate_block(slot_rows, gate_rows, put):
+        hit = dot(nt_dot(eye, slot_rows).astype(BF16), spread_e) == q_slot
+        rest = gate_rows
         for p in range(3):
-            gmat[l, p * n_tok:(p + 1) * n_tok, :] = jnp.where(hit, dot(parts[p], spread_e), 0.0).astype(BF16)
+            part = rest.astype(BF16)
+            rest = rest - part.astype(F32)
+            put(p, jnp.where(hit, dot(nt_dot(eye, part).astype(BF16), spread_e), 0.0).astype(BF16))
+
+    for n, m in enumerate((0, 3, 1)):
+        k = line_rows(mod(k_self + m))
+
+        def put_own(p, v, n=n):
+            gmat[n, p * n_tok:(p + 1) * n_tok, :] = v
+
+        gate_block(slots[k, :], gates[k, :], put_own)
+    wait_bytes(slots_far, n_r.at[0])
+    wait_bytes(gates_near, n_r.at[1])
+    for side in range(2):
+        for n in range(2):
+            near = mts[mod(k_self + (3 if side == 0 else 1))] if n == 0 else slots_far[side]
+
+            def put_near(p, v, side=side, n=n):
+                sel[side, p * n_tok:(p + 1) * n_tok, n * 256:n * 256 + both] = v
+
+            gate_block(near, gates_near[side, n], put_near)
     acc[...] = x_ref[...].astype(F32)
 
     def expert_up(l, cuts):
@@ -314,22 +367,50 @@
     def forward(l, c):
         with jax.named_scope('back_wait'):
             back_wait(l, c)
-        sendb[l, :, cols_at(c)] = dot(perm[...], y1[l, :, cols_at(c)]).astype(BF16)
-        for m in MATES:
-            home_copy(l, c, m).start()
-        y3[l, rows_at(k_self * home, home, 8), cols_at(c)] = sendb[l, rows_at(k_self * home, home, 8), cols_at(c)]
-
-    def collect(l, c):
-        with jax.named_scope('home_wait'):
-            wait_bytes(y3.at[l, pl.ds(0, (n_line - 1) * home), cols_at(c)], e_r.at[l, c])
-        part = dot(gmat[l], y3[l, :, cols_at(c)])
-        acc[:, cols_at(c)] += part[:n_tok] + part[n_tok:2 * n_tok] + part[2 * n_tok:]
-
-    def loop(body):
+        out = dot(perm[...], y1[l, :, cols_at(c)]).astype(BF16)
+        for s in range(n_line):
+            sendb[s >> 1, (s & 1) * both + l * home:(s & 1) * both + (l + 1) * home, cols_at(c)] = (
+                out[s * home:(s + 1) * home])
+        for m in (1, 3):
+            far_copy(l, c, m).start()
+        for m in (1, 3):
+            raw_copy(l, c, m).start()
+
+    def fold(v):
+        return v[:n_tok] + v[n_tok:2 * n_tok] + v[2 * n_tok:]
+
+    def home_rows(s):
+        return s >> 1, rows_at((s & 1) * both, both, 8)
+
+    def own_sums(c):
+        p, r = home_rows(k_self)
+        acc[:, cols_at(c)] += fold(dot(gmat[0], sendb[p, r, cols_at(c)]))
+        for side, m in ((0, 3), (1, 1)):
+            p, r = home_rows(mod(k_self + m))
+            part_out[:, side_cols(c, side)] = fold(
+                dot(sel[side, :, 0:both], sendb[p, r, side_cols(c, side)]))
+
+    def merge(c):
+        with jax.named_scope('far_wait'):
+            wait_bytes(y_far.at[:, cols_at(c)], f_r.at[c])
+        for side in range(2):
+            cols = side_cols(c, side)
+            part_out[:, cols] += fold(dot(sel[side, :, 256:256 + both], y_far[:, cols]))
+        for m in (1, 3):
+            sum_copy(c, m).start()
+
+    def collect(c):
+        with jax.named_scope('raw_wait'):
+            wait_bytes(y_raw.at[:, cols_at(c)], e_r.at[c])
+        for side in range(2):
+            cols = side_cols(c, side)
+            acc[:, cols] += fold(dot(gmat[1 + side], y_raw[:, cols]))
+
+    def loop(body, start=0, stop=n_chunk):
         def step(c, carry):
             body(c)
             return carry
-        lax.fori_loop(0, n_chunk, step, 0)
+        lax.fori_loop(start, stop, step, 0)
 
     expert_up(0, cuts[0])
     with jax.named_scope('down0'):
@@ -345,25 +426,44 @@
     with jax.named_scope('down1_forward0'):
         loop(down_and_forward)
 
-    def forward_and_collect(c):
+    def forward_and_sum(c):
         forward(1, c)
-        collect(0, c)
-
-    with jax.named_scope('forward1_collect0'):
-        loop(forward_and_collect)
+        own_sums(c)
+
+    def forward_and_merge(c):
+        forward_and_sum(c)
+        merge(c - lag)
+
+    with jax.named_scope('forward1'):
+        loop(forward_and_sum, 0, lag)
+        loop(forward_and_merge, lag, n_chunk)
+
+    def merge_and_collect(c):
+        merge(c)
+        collect(c - n_chunk + lag)
+
+    with jax.named_scope('merge'):
+        loop(merge_and_collect, n_chunk - lag, n_chunk)
+        loop(collect, lag, n_chunk)
+    wait_bytes(xg.at[pl.ds(0, (n_line - 1) * n_tok), :], g_s.at[0])
 
     def finish(c):
-        collect(1, c)
-        out_ref[:, cols_at(c)] = acc[:, cols_at(c)].astype(BF16)
-
-    with jax.named_scope('collect1'):
+        with jax.named_scope('sum_wait'):
+            wait_bytes(part_in.at[:, cols_at(c)], p_r.at[c])
+        x_ref[:, cols_at(c)] = (acc[:, cols_at(c)] + part_in[:, cols_at(c)]).astype(BF16)
+        pltpu.make_async_copy(x_ref.at[:, cols_at(c)], out_hbm.at[:, cols_at(c)], out_sem.at[0]).start()
+
+    with jax.named_scope('finish'):
         loop(finish)
 
     with jax.named_scope('drain'):
+        wait_bytes(x_ref, out_sem.at[0])
         wait_bytes(mts.at[pl.ds(0, n_line - 1)], mt_s.at[0])
-        wait_bytes(xg.at[pl.ds(0, (n_line - 1) * n_tok), :], g_s.at[0])
+        wait_bytes(slots_far, n_s.at[0])
+        wait_bytes(gates_near, n_s.at[1])
         wait_bytes(y1.at[:, pl.ds(0, others), :], c_s.at[0])
-        wait_bytes(y3.at[:, pl.ds(0, (n_line - 1) * home), :], e_s.at[0])
+        wait_bytes(y1.at[0], e_s.at[0])
+        wait_bytes(part_out, p_s.at[0])
 
 
 def solution(mesh):
@@ -379,16 +479,15 @@
         n_exp = n_loc * n_group
         cap = -(-(n_tok * n_top) // n_exp)
         n_rows = n_group * cap
-        n_half, n_chunk, f_tile, n_w2, cuts, ahead, lead = 5, 5, 256, 3, ((2, 4), (2, 4)), 5, 5
+        n_half, n_chunk, f_tile, n_w2, cuts, ahead, lag = 5, 5, 256, 3, ((2, 4), (2, 4)), 5, 3
         sem = pltpu.SemaphoreType.DMA
-        vmem = pl.BlockSpec(memory_space=pltpu.VMEM)
         hbm = pl.BlockSpec(memory_space=pl.ANY)
         n_dev = 2 * n_line
         return pl.pallas_call(
-            functools.partial(moe_kernel, n_line, cap, n_half, n_chunk, f_tile, cuts, ahead, lead),
+            functools.partial(moe_kernel, n_line, cap, n_half, n_chunk, f_tile, cuts, ahead, lag),
             out_shape=jax.ShapeDtypeStruct((n_tok, dim), BF16),
             in_specs=[hbm] * 6,
-            out_specs=vmem,
+            out_specs=hbm,
             scratch_shapes=[
                 pltpu.VMEM((n_tok, dim), BF16),
                 pltpu.VMEM((n_top, n_tok), jnp.int32),
@@ -396,7 +495,11 @@
                 pltpu.VMEM((n_loc, dim, ffn), BF16),
                 pltpu.VMEM((n_loc, dim, ffn), BF16),
                 pltpu.VMEM((n_w2, ffn, dim // n_chunk), BF16),
-                pltpu.VMEM((n_line, n_exp, n_tok), BF16),
+                pltpu.VMEM((n_exp, n_tok), BF16),
+                pltpu.VMEM((n_exp, n_tok), F32),
+                pltpu.VMEM((n_line, n_exp // n_line, n_tok), BF16),
+                pltpu.VMEM((2, n_exp // n_line, n_tok), BF16),
+                pltpu.VMEM((2, 2, n_exp // n_line, n_tok), F32),
                 pltpu.VMEM((n_line * n_tok, dim), BF16),
                 pltpu.VMEM((n_loc, n_rows, n_line * n_tok), BF16),
                 pltpu.VMEM((n_loc, n_rows, dim), BF16),
@@ -405,18 +508,24 @@
                 pltpu.VMEM((n_rows, ffn), F32),
                 pltpu.VMEM((n_rows, ffn), BF16),
                 pltpu.VMEM((n_loc, n_rows, dim), BF16),
-                pltpu.VMEM((n_loc, n_rows, dim), BF16),
+                pltpu.VMEM((n_loc * n_dev * cap, dim), BF16),
+                pltpu.VMEM((n_loc * n_dev * cap, dim), BF16),
                 pltpu.VMEM((n_rows, n_rows), BF16),
-                pltpu.VMEM((n_loc, 3 * n_tok, n_rows), BF16),
+                pltpu.VMEM((3, 3 * n_tok, n_loc * n_dev * cap), BF16),
+                pltpu.VMEM((n_tok, dim), F32),
+                pltpu.VMEM((n_tok, dim), F32),
                 pltpu.VMEM((n_tok, dim), F32),
                 sem((3,)),
+                sem((1,)),
                 sem((2, n_loc)),
                 sem((n_w2,)),
                 sem((1,)), sem((1,)),
+                sem((2,)), sem((2,)),
                 sem((1,)), sem((4, n_half)),
                 sem((1,)), sem((n_loc, n_half)),
                 sem((1,)), sem((n_loc, n_chunk)),
-                sem((1,)), sem((n_loc, n_chunk)),
+                sem((1,)), sem((n_chunk,)), sem((n_chunk,)),
+                sem((1,)), sem((n_chunk,)),
             ],
             compiler_params=pltpu.CompilerParams(
                 collective_id=0, has_side_effects=True, vmem_limit_bytes=67043328),

time: 88.9 us -> 84.7 us (0.953)
  Pallas kernels: 86.8 us -> 82.7 us
    pallas_call x1, Pallas kernels: 86.8 us -> 82.7 us  [device_step(): pl.pallas_call(functools.partial(moe_kernel, n_line, cap, n_half, n_chunk...]
where the time goes in v3:
time: 84.7 us; the launch traced here: 84.6 us
  Pallas kernels  82.7 us (98%)
  local copies, waits for them, and re-layouts  1.97 us (2%)
    pallas_call x1, Pallas kernels, device_step(): pl.pallas_call(functools.partial(moe_kernel, n_line, cap, n_half, n_chunk...  82.7 us
    unnamed x1, local copies, waits for them, and re-layouts  1.97 us

profile of v3, /device:TPU:97, one launch (start us, length us, event | category | flops | bytes accessed | tf_op | source)
XLA Modules:
  0.0 84.6 jit_solution(846260036275191850)
XLA Ops:
  0.0 82.7 %shard_map.64 = bf16[128,2560]{1,0:T(8,128)(2,1)} custom-call(bf16[128,2560]{1,0:T(8,128)(2,1)} %x_hbm.1, s32[6,128]{1,0:T(8,128)} %bitcast.2, f32[6,128]{1,0:T(8,128)} %bitcast.3, bf16[2,2560,1536]{2,1,0:T(8,128)(2,1)} %w1_hbm.1, bf16[2,2560,1536]{2,1,0:T(8,128)(2,1)} %w3_hbm.1, bf16[2,1536,2560]{2,1,0:T(8,128)(2,1)} %w2_hbm.1), custom_call_target="tpu_custom_call" | custom-call | tf_op jit(solution)/shard_map/pallas_call | solution.py:486
  82.7 2.0 %copy.8 = bf16[128,2560]{1,0:T(8,128)(2,1)} copy(bf16[128,2560]{1,0:T(8,128)(2,1)} %shard_map.64) | data formatting | bytes 1310720

commit v4 on v3

--- a/solution.py
+++ b/solution.py
@@ -27,11 +27,11 @@
 
 
 def moe_kernel(
-    n_line, cap, n_half, n_chunk, f_tile, cuts, ahead, lag,
-    x_hbm, idx_hbm, gate_hbm, w1_hbm, w3_hbm, w2_hbm, out_hbm,
+    n_line, cap, n_half, n_chunk, f_tile, cuts, ahead, lead, lag,
+    x_hbm, idx_hbm, gate_hbm, w1_hbm, w3_hbm, w2_hbm, out_ref,
     x_ref, idx_ref, gate_ref, w1, w3, w2, slots, gates, mts, slots_far, gates_near, xg, sel, sendb, rows, part_a, part_b, hid, y1,
     y_raw, y_far, perm, gmat, acc, part_out, part_in,
-    in_sem, out_sem, w13_sem, w2_sem, mt_s, mt_r, n_s, n_r, g_s, g_r, d_s, d_r, c_s, c_r, e_s, e_r, f_r, p_s, p_r,
+    in_sem, w13_sem, w2_sem, mt_s, mt_r, n_s, n_r, g_s, g_r, d_s, d_r, c_s, c_r, e_s, e_r, f_r, p_s, p_r,
 ):
     n_tok, dim = x_ref.shape
     n_top = idx_ref.shape[0]
@@ -264,21 +264,27 @@
             gather_copy(m, h).wait_recv()
             relay_copy(m, h).start()
 
+    def gathered(h):
+        with jax.named_scope('gather_wait'):
+            for m in (1, 3):
+                relay_copy(m, h).wait_recv()
+        with jax.named_scope('spread_send'):
+            spread(0, h)
+
     with jax.named_scope('gather_and_spread'):
         for h in range(n_half):
             relay(h)
             if h + ahead < n_half:
                 for m in (1, 3):
                     gather_copy(m, h + ahead).start()
+            if h >= lead - 1:
+                gathered(h - lead + 1)
         for m in (1, 3):
             for copy in note_copies(m):
                 copy.start()
-        for h in range(n_half):
-            with jax.named_scope('gather_wait'):
-                for m in (1, 3):
-                    relay_copy(m, h).wait_recv()
-            with jax.named_scope('spread_send'):
-                spread(0, h)
+        for h in range(n_half - lead + 1, n_half):
+            gathered(h)
+
     with jax.named_scope('spread_rest'):
         for h in range(n_half):
             for l in range(1, n_loc):
@@ -288,39 +294,6 @@
     o_in = (o12 & 7) * per + (o12 >> 3) * cap + (r - r12 * cap)
     perm[...] = (lax.broadcasted_iota(jnp.int32, (n_rows, n_rows), 1) == o_in).astype(BF16)
 
-    eye = (lax.broadcasted_iota(jnp.int32, (n_tok, n_tok), 0)
-           == lax.broadcasted_iota(jnp.int32, (n_tok, n_tok), 1)).astype(BF16)
-    q = lax.broadcasted_iota(jnp.int32, (1, both), 1)
-    q12 = div12(q)
-    q_slot = (q - q12 * cap).astype(F32)
-    q_exp = n_loc * (q12 & 7) + (q12 >> 3)
-    spread_e = (lax.broadcasted_iota(jnp.int32, (n_line_exp, both), 0) == q_exp).astype(BF16)
-
-    def gate_block(slot_rows, gate_rows, put):
-        hit = dot(nt_dot(eye, slot_rows).astype(BF16), spread_e) == q_slot
-        rest = gate_rows
-        for p in range(3):
-            part = rest.astype(BF16)
-            rest = rest - part.astype(F32)
-            put(p, jnp.where(hit, dot(nt_dot(eye, part).astype(BF16), spread_e), 0.0).astype(BF16))
-
-    for n, m in enumerate((0, 3, 1)):
-        k = line_rows(mod(k_self + m))
-
-        def put_own(p, v, n=n):
-            gmat[n, p * n_tok:(p + 1) * n_tok, :] = v
-
-        gate_block(slots[k, :], gates[k, :], put_own)
-    wait_bytes(slots_far, n_r.at[0])
-    wait_bytes(gates_near, n_r.at[1])
-    for side in range(2):
-        for n in range(2):
-            near = mts[mod(k_self + (3 if side == 0 else 1))] if n == 0 else slots_far[side]
-
-            def put_near(p, v, side=side, n=n):
-                sel[side, p * n_tok:(p + 1) * n_tok, n * 256:n * 256 + both] = v
-
-            gate_block(near, gates_near[side, n], put_near)
     acc[...] = x_ref[...].astype(F32)
 
     def expert_up(l, cuts):
@@ -426,6 +399,40 @@
     with jax.named_scope('down1_forward0'):
         loop(down_and_forward)
 
+    with jax.named_scope('gate_blocks'):
+        eye = (lax.broadcasted_iota(jnp.int32, (n_tok, n_tok), 0)
+               == lax.broadcasted_iota(jnp.int32, (n_tok, n_tok), 1)).astype(BF16)
+        q = lax.broadcasted_iota(jnp.int32, (1, both), 1)
+        q12 = div12(q)
+        q_slot = (q - q12 * cap).astype(F32)
+        q_exp = n_loc * (q12 & 7) + (q12 >> 3)
+        spread_e = (lax.broadcasted_iota(jnp.int32, (n_line_exp, both), 0) == q_exp).astype(BF16)
+
+        def gate_block(slot_rows, gate_rows, put):
+            hit = dot(nt_dot(eye, slot_rows).astype(BF16), spread_e) == q_slot
+            rest = gate_rows
+            for p in range(3):
+                part = rest.astype(BF16)
+                rest = rest - part.astype(F32)
+                put(p, jnp.where(hit, dot(nt_dot(eye, part).astype(BF16), spread_e), 0.0).astype(BF16))
+
+        for n, m in enumerate((0, 3, 1)):
+            k = line_rows(mod(k_self + m))
+
+            def put_own(p, v, n=n):
+                gmat[n, p * n_tok:(p + 1) * n_tok, :] = v
+
+            gate_block(slots[k, :], gates[k, :], put_own)
+        wait_bytes(slots_far, n_r.at[0])
+        wait_bytes(gates_near, n_r.at[1])
+        for side in range(2):
+            for n in range(2):
+                near = mts[mod(k_self + (3 if side == 0 else 1))] if n == 0 else slots_far[side]
+
+                def put_near(p, v, side=side, n=n):
+                    sel[side, p * n_tok:(p + 1) * n_tok, n * 256:n * 256 + both] = v
+
+                gate_block(near, gates_near[side, n], put_near)
     def forward_and_sum(c):
         forward(1, c)
         own_sums(c)
@@ -450,14 +457,12 @@
     def finish(c):
         with jax.named_scope('sum_wait'):
             wait_bytes(part_in.at[:, cols_at(c)], p_r.at[c])
-        x_ref[:, cols_at(c)] = (acc[:, cols_at(c)] + part_in[:, cols_at(c)]).astype(BF16)
-        pltpu.make_async_copy(x_ref.at[:, cols_at(c)], out_hbm.at[:, cols_at(c)], out_sem.at[0]).start()
+        out_ref[:, cols_at(c)] = (acc[:, cols_at(c)] + part_in[:, cols_at(c)]).astype(BF16)
 
     with jax.named_scope('finish'):
         loop(finish)
 
     with jax.named_scope('drain'):
-        wait_bytes(x_ref, out_sem.at[0])
         wait_bytes(mts.at[pl.ds(0, n_line - 1)], mt_s.at[0])
         wait_bytes(slots_far, n_s.at[0])
         wait_bytes(gates_near, n_s.at[1])
@@ -479,15 +484,15 @@
         n_exp = n_loc * n_group
         cap = -(-(n_tok * n_top) // n_exp)
         n_rows = n_group * cap
-        n_half, n_chunk, f_tile, n_w2, cuts, ahead, lag = 5, 5, 256, 3, ((2, 4), (2, 4)), 5, 3
+        n_half, n_chunk, f_tile, n_w2, cuts, ahead, lead, lag = 5, 5, 256, 3, ((2, 4), (2, 4)), 4, 3, 3
         sem = pltpu.SemaphoreType.DMA
         hbm = pl.BlockSpec(memory_space=pl.ANY)
         n_dev = 2 * n_line
         return pl.pallas_call(
-            functools.partial(moe_kernel, n_line, cap, n_half, n_chunk, f_tile, cuts, ahead, lag),
-            out_shape=jax.ShapeDtypeStruct((n_tok, dim), BF16),
+            functools.partial(moe_kernel, n_line, cap, n_half, n_chunk, f_tile, cuts, ahead, lead, lag),
+            out_shape=pltpu.VMEM((n_tok, dim), BF16),
             in_specs=[hbm] * 6,
-            out_specs=hbm,
+            out_specs=pl.BlockSpec(memory_space=pltpu.VMEM),
             scratch_shapes=[
                 pltpu.VMEM((n_tok, dim), BF16),
                 pltpu.VMEM((n_top, n_tok), jnp.int32),
@@ -516,7 +521,6 @@
                 pltpu.VMEM((n_tok, dim), F32),
                 pltpu.VMEM((n_tok, dim), F32),
                 sem((3,)),
-                sem((1,)),
                 sem((2, n_loc)),
                 sem((n_w2,)),
                 sem((1,)), sem((1,)),
@@ -528,7 +532,7 @@
                 sem((1,)), sem((n_chunk,)),
             ],
             compiler_params=pltpu.CompilerParams(
-                collective_id=0, has_side_effects=True, vmem_limit_bytes=67043328),
+                collective_id=0, has_side_effects=True, vmem_limit_bytes=66300000),
         )(tokens, expert_ids.T, gates.T, w_gate, w_up, w_down)
 
     return jax.shard_map(

time: 84.7 us -> 82.7 us (0.976)
  local copies, waits for them, and re-layouts: 1.97 us -> 0.84 us
  Pallas kernels: 82.7 us -> 81.8 us
    unnamed x1, local copies, waits for them, and re-layouts: 1.97 us -> 0.84 us
    pallas_call x1, Pallas kernels: 82.7 us -> 81.8 us  [device_step(): pl.pallas_call(functools.partial(moe_kernel, n_line, cap, n_half, n_chunk...]
where the time goes in v4:
time: 82.7 us; the launch traced here: 82.6 us
  Pallas kernels  81.8 us (99%)
  local copies, waits for them, and re-layouts  0.84 us (1%)
    pallas_call x1, Pallas kernels, device_step(): pl.pallas_call(functools.partial(moe_kernel, n_line, cap, n_half, n_chunk...  81.8 us

profile of v4, /device:TPU:97, one launch (start us, length us, event | category | flops | bytes accessed | tf_op | source)
XLA Modules:
  0.0 82.6 jit_solution(10560289042335306524)
XLA Ops:
  0.0 81.8 %shard_map.64 = bf16[128,2560]{1,0:T(8,128)(2,1)S(1)} custom-call(bf16[128,2560]{1,0:T(8,128)(2,1)} %x_hbm.1, s32[6,128]{1,0:T(8,128)} %bitcast.2, f32[6,128]{1,0:T(8,128)} %bitcast.3, bf16[2,2560,1536]{2,1,0:T(8,128)(2,1)} %w1_hbm.1, bf16[2,2560,1536]{2,1,0:T(8,128)(2,1)} %w3_hbm.1, bf16[2,1536,2560]{2,1,0:T(8,128)(2,1)} %w2_hbm.1), custom_call_target="tpu_custom_call" | custom-call | tf_op jit(solution)/shard_map/pallas_call | solution.py:491
  81.8 0.8 %copy.8 = bf16[128,2560]{1,0:T(8,128)(2,1)} copy(bf16[128,2560]{1,0:T(8,128)(2,1)S(1)} %shard_map.64) | data formatting | bytes 1310720

commit v5 on v4

--- a/solution.py
+++ b/solution.py
@@ -10,7 +10,7 @@
 MESH = pl.DeviceIdType.MESH
 F32 = jnp.float32
 BF16 = jnp.bfloat16
-PEERS = [(1, 0), (3, 0), (1, 1), (3, 1), (2, 0), (2, 1), (0, 1)]
+PEERS = [(2, 0), (2, 1), (1, 0), (3, 0), (1, 1), (3, 1), (0, 1)]
 MATES = [1, 3, 2]
 
 
@@ -119,7 +119,7 @@
 
     def back_targets():
         out = []
-        for m in (1, 3, 2):
+        for m in (2, 1, 3):
             for side in (0, 1):
                 pos = mod((yy if side else xx) + m)
                 dev = (dp, pos, xx * 2 + 1) if side else (dp, yy, pos * 2)
@@ -237,6 +237,13 @@
             gather_copy(m, h).start()
 
     xg[rows_at(k_self * n_tok, n_tok, 8), :] = x_ref[...]
+
+    def relay(h):
+        for m in (1, 3):
+            gather_copy(m, h).wait_recv()
+            relay_copy(m, h).start()
+
+    relay(0)
 
     r = lax.broadcasted_iota(jnp.int32, (n_rows, 1), 0)
     r12 = div12(r)
@@ -259,10 +266,6 @@
             spread_copy(l, h, m, dc).start()
         rows[l, rows_at(i_self * per, per, 8), half_cols(h)] = sendb[l, rows_at(d_self * per, per, 8), half_cols(h)]
 
-    def relay(h):
-        for m in (1, 3):
-            gather_copy(m, h).wait_recv()
-            relay_copy(m, h).start()
 
     def gathered(h):
         with jax.named_scope('gather_wait'):
@@ -273,7 +276,8 @@
 
     with jax.named_scope('gather_and_spread'):
         for h in range(n_half):
-            relay(h)
+            if h > 0:
+                relay(h)
             if h + ahead < n_half:
                 for m in (1, 3):
                     gather_copy(m, h + ahead).start()

time: 82.7 us -> 82.4 us (level)
  no operation moved by 1% of the time
where the time goes in v5:
time: 82.4 us
  Pallas kernels  81.5 us (99%)
  local copies, waits for them, and re-layouts  0.84 us (1%)
    pallas_call x1, Pallas kernels, device_step(): pl.pallas_call(functools.partial(moe_kernel, n_line, cap, n_half, n_chunk...  81.5 us

profile of v5, /device:TPU:97, one launch (start us, length us, event | category | flops | bytes accessed | tf_op | source)
XLA Modules:
  0.0 82.4 jit_solution(8803537127910348970)
XLA Ops:
  0.0 81.5 %shard_map.64 = bf16[128,2560]{1,0:T(8,128)(2,1)S(1)} custom-call(bf16[128,2560]{1,0:T(8,128)(2,1)} %x_hbm.1, s32[6,128]{1,0:T(8,128)} %bitcast.2, f32[6,128]{1,0:T(8,128)} %bitcast.3, bf16[2,2560,1536]{2,1,0:T(8,128)(2,1)} %w1_hbm.1, bf16[2,2560,1536]{2,1,0:T(8,128)(2,1)} %w3_hbm.1, bf16[2,1536,2560]{2,1,0:T(8,128)(2,1)} %w2_hbm.1), custom_call_target="tpu_custom_call" | custom-call | tf_op jit(solution)/shard_map/pallas_call | solution.py:495
  81.5 0.8 %copy.8 = bf16[128,2560]{1,0:T(8,128)(2,1)} copy(bf16[128,2560]{1,0:T(8,128)(2,1)S(1)} %shard_map.64) | data formatting | bytes 1310720

commit v6 on v5

--- a/solution.py
+++ b/solution.py
@@ -10,6 +10,7 @@
 MESH = pl.DeviceIdType.MESH
 F32 = jnp.float32
 BF16 = jnp.bfloat16
+BF16_MAX = float(jnp.finfo(jnp.bfloat16).max)
 PEERS = [(2, 0), (2, 1), (1, 0), (3, 0), (1, 1), (3, 1), (0, 1)]
 MATES = [1, 3, 2]
 
@@ -416,7 +417,7 @@
             hit = dot(nt_dot(eye, slot_rows).astype(BF16), spread_e) == q_slot
             rest = gate_rows
             for p in range(3):
-                part = rest.astype(BF16)
+                part = jnp.minimum(rest, BF16_MAX).astype(BF16)
                 rest = rest - part.astype(F32)
                 put(p, jnp.where(hit, dot(nt_dot(eye, part).astype(BF16), spread_e), 0.0).astype(BF16))
 

time: 82.4 us -> 82.4 us (level)
  no operation moved by 1% of the time
where the time goes in v6:
time: 82.4 us
  Pallas kernels  81.5 us (99%)
  local copies, waits for them, and re-layouts  0.84 us (1%)
    pallas_call x1, Pallas kernels, device_step(): pl.pallas_call(functools.partial(moe_kernel, n_line, cap, n_half, n_chunk...  81.5 us

profile of v6, /device:TPU:97, one launch (start us, length us, event | category | flops | bytes accessed | tf_op | source)
XLA Modules:
  0.0 82.4 jit_solution(5776817608250400284)
XLA Ops:
  0.0 81.5 %shard_map.64 = bf16[128,2560]{1,0:T(8,128)(2,1)S(1)} custom-call(bf16[128,2560]{1,0:T(8,128)(2,1)} %x_hbm.1, s32[6,128]{1,0:T(8,128)} %bitcast.2, f32[6,128]{1,0:T(8,128)} %bitcast.3, bf16[2,2560,1536]{2,1,0:T(8,128)(2,1)} %w1_hbm.1, bf16[2,2560,1536]{2,1,0:T(8,128)(2,1)} %w3_hbm.1, bf16[2,1536,2560]{2,1,0:T(8,128)(2,1)} %w2_hbm.1), custom_call_target="tpu_custom_call" | custom-call | tf_op jit(solution)/shard_map/pallas_call | solution.py:496
  81.5 0.8 %copy.8 = bf16[128,2560]{1,0:T(8,128)(2,1)} copy(bf16[128,2560]{1,0:T(8,128)(2,1)S(1)} %shard_map.64) | data formatting | bytes 1310720

commit v7 on v6

--- a/solution.py
+++ b/solution.py
@@ -101,7 +101,7 @@
         side = m // 2
         block = xg.at[rows_at(mod(k_self - m) * n_tok + side * (n_tok // 2), n_tok // 2, 8), half_cols(h)]
         return pltpu.make_async_remote_copy(
-            block, block, g_s.at[0], g_r.at[2 + side, h], device_id=mate(m), device_id_type=MESH)
+            block, block, g_s.at[0], g_r.at[2, h], device_id=mate(m), device_id_type=MESH)
 
     def wait_bytes(ref, sem):
         pltpu.make_async_copy(ref, ref, sem).wait()
@@ -111,12 +111,15 @@
         return pltpu.make_async_remote_copy(
             sendb.at[l, rows_at(d * per, per, 8), half_cols(h)],
             rows.at[l, rows_at(i_self * per, per, 8), half_cols(h)],
-            d_s.at[0], d_r.at[l, h], device_id=dev, device_id_type=MESH)
+            d_s.at[0], d_r.at[l, group_of(l, h)], device_id=dev, device_id_type=MESH)
 
     others = (2 * n_line - 1) * per
 
-    def spread_wait(l, h):
-        wait_bytes(rows.at[l, pl.ds(0, others), half_cols(h)], d_r.at[l, h])
+    def group_of(l, h):
+        return sum(h >= edge for edge in cuts[l])
+
+    def spread_wait(l, h0, h1):
+        wait_bytes(rows.at[l, pl.ds(0, others), pl.ds(h0 * half, (h1 - h0) * half)], d_r.at[l, group_of(l, h0)])
 
     def back_targets():
         out = []
@@ -270,8 +273,7 @@
 
     def gathered(h):
         with jax.named_scope('gather_wait'):
-            for m in (1, 3):
-                relay_copy(m, h).wait_recv()
+            wait_bytes(xg.at[pl.ds(0, n_tok), half_cols(h)], g_r.at[2, h])
         with jax.named_scope('spread_send'):
             spread(0, h)
 
@@ -308,8 +310,7 @@
         edges = (0,) + cuts + (n_half,)
         for h0, h1 in zip(edges, edges[1:]):
             with jax.named_scope('spread_wait'):
-                for h in range(h0, h1):
-                    spread_wait(l, h)
+                spread_wait(l, h0, h1)
             k = slice(h0 * half, h1 * half)
 
             def tile(n, carry, h0=h0, h1=h1, k=k):
@@ -530,8 +531,8 @@
                 sem((n_w2,)),
                 sem((1,)), sem((1,)),
                 sem((2,)), sem((2,)),
-                sem((1,)), sem((4, n_half)),
-                sem((1,)), sem((n_loc, n_half)),
+                sem((1,)), sem((3, n_half)),
+                sem((1,)), sem((n_loc, 1 + max(len(edges) for edges in cuts))),
                 sem((1,)), sem((n_loc, n_chunk)),
                 sem((1,)), sem((n_chunk,)), sem((n_chunk,)),
                 sem((1,)), sem((n_chunk,)),

time: 82.4 us -> 82.4 us (level)
  no operation moved by 1% of the time
where the time goes in v7:
time: 82.4 us; the launch traced here: 82.3 us
  Pallas kernels  81.4 us (99%)
  local copies, waits for them, and re-layouts  0.84 us (1%)
    pallas_call x1, Pallas kernels, device_step(): pl.pallas_call(functools.partial(moe_kernel, n_line, cap, n_half, n_chunk...  81.4 us

profile of v7, /device:TPU:97, one launch (start us, length us, event | category | flops | bytes accessed | tf_op | source)
XLA Modules:
  0.0 82.3 jit_solution(6618946736633634979)
XLA Ops:
  0.0 81.4 %shard_map.64 = bf16[128,2560]{1,0:T(8,128)(2,1)S(1)} custom-call(bf16[128,2560]{1,0:T(8,128)(2,1)} %x_hbm.1, s32[6,128]{1,0:T(8,128)} %bitcast.2, f32[6,128]{1,0:T(8,128)} %bitcast.3, bf16[2,2560,1536]{2,1,0:T(8,128)(2,1)} %w1_hbm.1, bf16[2,2560,1536]{2,1,0:T(8,128)(2,1)} %w3_hbm.1, bf16[2,1536,2560]{2,1,0:T(8,128)(2,1)} %w2_hbm.1), custom_call_target="tpu_custom_call" | custom-call | tf_op jit(solution)/shard_map/pallas_call | solution.py:497
  81.4 0.8 %copy.8 = bf16[128,2560]{1,0:T(8,128)(2,1)} copy(bf16[128,2560]{1,0:T(8,128)(2,1)S(1)} %shard_map.64) | data formatting | bytes 1310720
